TPU v7x, 32 devices: a whole 2x2x4 slice. The times are simulated.
32 devices in a mesh: band: 16 (over z, y, x), ch: 2 (over core).
Axes of the slice: x: 2, y: 2, z: 4, core: 2. Of those that a mesh axis runs over, the one named last changes fastest.
Arguments:
- grid_field: bfloat16 [100, 262144], P(None, 'band'), may hold values from -6 to 6
- band_points: int32 [16], P('band'), may hold values from 8192 to 16384
- block_ids: int32 [16, 16], P('band'), may hold values from 0 to 511, as said below
- block_count: int32 [16], P('band'), may hold values from 8 to 16
- block_weight: bfloat16 [16, 16, 256, 512], P('band'), may hold values from 0 to 0.039794922
- embed_weight: bfloat16 [100, 1024], P(None, 'ch'), may hold values from -0.3125 to 0.3125
- edge_src: int32 [81920], P('band'), may hold values from 0 to 4095, as said below
- edge_dst: int32 [81920], P('band'), may hold values from 0 to 4095, as said below
- edge_in_weight: bfloat16 [2, 1024, 1024], P(None, None, 'ch'), may hold values from -0.1875 to 0.1875
- edge_out_weight: bfloat16 [1024, 1024], P('ch'), may hold values from -0.0625 to 0.0625
- node_in_weight: bfloat16 [2, 1024, 1024], P(None, None, 'ch'), may hold values from -0.125 to 0.125
- node_out_weight: bfloat16 [1024, 1024], P('ch'), may hold values from -0.1875 to 0.1875
Outputs:
- node_state: bfloat16 [4096, 1024], P('band', 'ch')
Inputs may be any that keep to these rules, and one draw needn't show every extreme that they name: For band b, block_ids[b, k] * 512 lies from max(b * 16384 - 16384 // 2, 0) to min((b + 1) * 16384 + 16384 // 2, 262144) - 512; both ends are named by every band; ids may repeat. `edge_src`: edge e belongs to band b = e // 5120; its source node lies in bands b - 1 to b + 1 of the mesh. `edge_dst`: edge e ends at a node of its band b = e // 5120.
All inputs are finite; a program needn't handle non-finite values.
Results may differ from a plain program's by a relative error of at most 0.015.
Values may be sent and summed in bfloat16 or wider, within the bound.
A program may use at most 64 MiB of HBM per device.

v0:
```python
import jax
import jax.numpy as jnp
from jax import lax
from jax.sharding import PartitionSpec as P


def extended_2(block, sides, width):
    for axis, dim in sides:
        count = lax.axis_size(axis)
        forward = [(i, i + 1) for i in range(count - 1)]
        backward = [(target, source) for source, target in forward]
        low = lax.ppermute(
            lax.slice_in_dim(block, block.shape[dim] - width, None, axis=dim), axis, forward
        )
        high = lax.ppermute(lax.slice_in_dim(block, 0, width, axis=dim), axis, backward)
        block = jnp.concatenate([low, block, high], axis=dim)
    return block


def on_device(
    grid_field,
    band_points,
    block_ids,
    block_count,
    block_weight,
    embed_weight,
    edge_src,
    edge_dst,
    edge_in_weight,
    edge_out_weight,
    node_in_weight,
    node_out_weight,
):
    band_index = lax.axis_index("band")
    channels, points = grid_field.shape
    kblocks = block_weight.shape[1]
    node_count = block_weight.shape[2]
    block_len = block_weight.shape[3]
    sub_count = points // block_len
    column = lax.broadcasted_iota(jnp.int32, (1, points), 1)
    live = jnp.where(column < band_points[0], grid_field, jnp.zeros_like(grid_field))
    share = channels // lax.axis_size("ch")
    local_live = lax.dynamic_slice_in_dim(live, lax.axis_index("ch") * share, share, 0)
    extended = extended_2(local_live, (("band", 1),), points)
    first_block = (band_index - 1) * sub_count
    ext_blocks = extended.shape[1] // block_len
    tiles = extended.reshape(extended.shape[0], ext_blocks, block_len)
    local_ids = block_ids[0] - first_block
    tile_ids = lax.broadcasted_iota(jnp.int32, (kblocks, ext_blocks), 1)
    slot_live = lax.broadcasted_iota(jnp.int32, (kblocks, ext_blocks), 0) < block_count[0]
    selector = ((local_ids[:, None] == tile_ids) & slot_live).astype(jnp.bfloat16)
    blocks = jnp.einsum("ks,csp->kcp", selector, tiles, preferred_element_type=jnp.float32).astype(
        jnp.bfloat16
    )
    remapped = jnp.einsum(
        "knp,kcp->nc", block_weight[0], blocks, preferred_element_type=jnp.float32
    ).astype(jnp.bfloat16)
    remapped = lax.all_gather(remapped, "ch", axis=1, tiled=True)
    initial = jnp.dot(remapped, embed_weight, preferred_element_type=jnp.float32).astype(
        jnp.bfloat16
    )
    shard_part = lax.all_gather(initial, "ch", axis=1, tiled=True)
    rows_src = edge_in_weight[0]
    rows_dst = edge_in_weight[1]
    rows_node = node_in_weight[0]
    source_acc = jnp.dot(shard_part, rows_src, preferred_element_type=jnp.float32)
    target_acc = jnp.dot(shard_part, rows_dst, preferred_element_type=jnp.float32)
    direct = jnp.dot(shard_part, rows_node, preferred_element_type=jnp.float32)
    source_proj = source_acc.astype(jnp.bfloat16)
    target_proj = target_acc.astype(jnp.bfloat16)
    source_ext = extended_2(source_proj, (("band", 0),), node_count)
    src_local = edge_src - (band_index - 1) * node_count
    dst_local = edge_dst - band_index * node_count
    pre_act = jnp.take(source_ext, src_local, axis=0).astype(jnp.float32) + jnp.take(
        target_proj, dst_local, axis=0
    ).astype(jnp.float32)
    edge_hidden = jax.nn.silu(pre_act).astype(jnp.bfloat16)
    messages = jnp.dot(edge_hidden, edge_out_weight, preferred_element_type=jnp.float32)
    node_ids = lax.broadcasted_iota(jnp.int32, (node_count, 1), 0)
    onehot = (dst_local[None, :] == node_ids).astype(jnp.float32)
    partial_agg = jnp.dot(
        onehot, messages, preferred_element_type=jnp.float32, precision=lax.Precision.HIGHEST
    )
    agg_half = lax.psum_scatter(
        partial_agg.astype(jnp.bfloat16), "ch", scatter_dimension=1, tiled=True
    )
    rows_agg = node_in_weight[1]
    from_agg = jnp.dot(
        lax.all_gather(agg_half, "ch", axis=1, tiled=True),
        rows_agg,
        preferred_element_type=jnp.float32,
    )
    update = jax.nn.silu(direct + from_agg).astype(jnp.bfloat16)
    partial_out = jnp.dot(update, node_out_weight, preferred_element_type=jnp.float32)
    summed = lax.psum_scatter(
        partial_out.astype(jnp.bfloat16), "ch", scatter_dimension=1, tiled=True
    ).astype(jnp.float32)
    return (initial.astype(jnp.float32) + summed).astype(jnp.bfloat16)


def solution(mesh):
    return jax.shard_map(
        on_device,
        mesh=mesh,
        in_specs=(
            P(None, "band"),
            P("band"),
            P("band", None),
            P("band"),
            P("band", None, None, None),
            P(None, "ch"),
            P("band"),
            P("band"),
            P(None, None, "ch"),
            P("ch", None),
            P(None, None, "ch"),
            P("ch", None),
        ),
        out_specs=P("band", "ch"),
        check_vma=False,
    )
```

profile of v0, /device:TPU:0, one launch (start us, length us, event | category | flops | bytes accessed | tf_op | source)
XLA Modules:
  0.0 218.2 jit_solution(12552808239125155742)
XLA Ops:
  6.5 0.0 copy-start
  6.5 0.0 reduce-scatter.3.cloned.1.call-start
  7.3 2.2 %dynamic-slice_select_fusion = bf16[50,16384]{1,0:T(8,128)(2,1)S(1)} fusion(bf16[100,16384]{1,0:T(8,128)(2,1)} %param.12, s32[]{:T(128)S(6)} %select_n.25, pred[16384]{0:T(1024)(128)(4,1)S(1)} %iota_compare_fusion.4), kind=kLoop, calls=%fused_computation.18 | loop fusion | flops 819200 | bytes 3293188 | tf_op jit(solution)/shard_map/jit(_where)/select_n | solution.py:41
  9.5 1.3 collective-permute-start.1
  10.8 6.8 %collective-permute-start = (bf16[50,16384]{1,0:T(8,128)(2,1)S(1)}, bf16[50,16384]{1,0:T(8,128)(2,1)}, u32[]{:S(2)}, u32[]{:S(2)}) collective-permute-start(bf16[50,16384]{1,0:T(8,128)(2,1)S(1)} %dynamic-slice_select_fusion), channel_id=1, source_target_pairs={{0,2},{2,4},{4,6},{6,8},{8,10},{10,12},{12,14},{14,16},{16,18},{18... | collective-permute-start | bytes 4915208 | tf_op jit(solution)/shard_map/ppermute | solution.py:12
  18.2 0.7 subtract_bitcast_fusion
  18.9 0.7 fusion.42
  19.6 0.8 compare_and_fusion
  20.4 34.9 %collective-permute-done.1 = bf16[50,16384]{1,0:T(8,128)(2,1)} collective-permute-done((bf16[50,16384]{1,0:T(8,128)(2,1)S(1)}, bf16[50,16384]{1,0:T(8,128)(2,1)}, u32[]{:S(2)}, u32[]{:S(2)}) %collective-permute-start.1) | collective-permute-done | bytes 1638432 | tf_op jit(solution)/shard_map/ppermute | solution.py:15
  55.3 39.4 %collective-permute-done = bf16[50,16384]{1,0:T(8,128)(2,1)} collective-permute-done((bf16[50,16384]{1,0:T(8,128)(2,1)S(1)}, bf16[50,16384]{1,0:T(8,128)(2,1)}, u32[]{:S(2)}, u32[]{:S(2)}) %collective-permute-start) | collective-permute-done | bytes 1638432 | tf_op jit(solution)/shard_map/ppermute | solution.py:12
  94.7 2.4 %pad_maximum_fusion = bf16[50,49152]{1,0:T(8,128)(2,1)S(1)} fusion(bf16[50,16384]{1,0:T(8,128)(2,1)} %collective-permute-done.1, bf16[50,16384]{1,0:T(8,128)(2,1)S(1)} %dynamic-slice_select_fusion, bf16[50,16384]{1,0:T(8,128)(2,1)} %collective-permute-done), kind=kLoop, calls=%fused_computation.3 | loop fusion | flops 14745600 | bytes 9830400 | tf_op jit(solution)/shard_map/concatenate | solution.py:16
  97.1 2.1 copy.14
  99.2 0.0 copy-start.2
  99.3 0.0 copy-start.3
  99.3 0.8 fusion.13
  100.1 1.4 copy-done.2
  101.4 1.4 fusion.23
  102.8 1.8 all-gather
  104.7 0.0 copy-done.3
  104.7 0.2 convolution_convert_fusion.3
  105.0 2.2 all_gather.10
  107.2 1.7 convolution_convert_fusion.2
  108.8 1.3 collective-permute-start.3
  110.1 5.1 %collective-permute-start.2 = (bf16[256,512]{1,0:T(8,128)(2,1)S(1)}, bf16[256,512]{1,0:T(8,128)(2,1)S(1)}, u32[]{:S(2)}, u32[]{:S(2)}) collective-permute-start(bf16[256,512]{1,0:T(8,128)(2,1)S(1)} %convolution_convert_fusion.2), channel_id=1, source_target_pairs={{0,2},{2,4},{4,6},{6,8},{8,10},{10,12},{12,14},{14,16},{16,18},{18... | collective-permute-start | bytes 786440 | tf_op jit(solution)/shard_map/ppermute | solution.py:12
  115.3 1.7 convolution_convert_fusion.1
  116.9 21.5 %gather_fusion.1 = bf16[5120,512]{1,0:T(8,128)(2,1)} fusion(bf16[256,512]{1,0:T(8,128)(2,1)S(1)} %convolution_convert_fusion.1, s32[5120]{0:T(1024)S(1)} %fusion.41), kind=kCustom, calls=%fused_computation.1 | custom fusion | bytes 10506240 | tf_op jit(solution)/shard_map/jit(_take)/gather | solution.py:74
  138.4 0.0 collective-permute-done.3
  138.4 0.0 collective-permute-done.2
  138.4 0.1 pad_maximum_fusion.1
  138.5 21.5 %gather_fusion = bf16[5120,512]{1,0:T(8,128)(2,1)} fusion(bf16[768,512]{1,0:T(8,128)(2,1)S(1)} %pad_maximum_fusion.1, s32[5120]{0:T(1024)S(1)} %fusion.42), kind=kCustom, calls=%fused_computation | custom fusion | bytes 10506240 | tf_op jit(solution)/shard_map/jit(_take)/gather | solution.py:74
  159.9 0.0 copy-done
  159.9 12.4 %fusion = f32[5120,1024]{1,0:T(8,128)S(1)} fusion(bf16[512,1024]{1,0:T(8,128)(2,1)S(1)} %copy-done, bf16[5120,512]{1,0:T(8,128)(2,1)} %gather_fusion.1, bf16[5120,512]{1,0:T(8,128)(2,1)} %gather_fusion, pred[5120]{0:T(1024)(128)(4,1)S(1)} %get-tuple-element.5, pred[5120]{0:T(1024)(128)(4,1)S(1)} %get-tuple-element.7), kind=kOutput, calls=%fused_computation.4 | convolution fusion | flops 5394923520 | bytes 32516096 | tf_op jit(solution)/shard_map/dot_general | solution.py:78
  172.3 0.0 copy-start.4
  172.3 14.0 %fusion.16 = bf16[256,1024]{1,0:T(8,128)(2,1)} fusion(f32[5120,1024]{1,0:T(8,128)S(1)} %fusion, s32[5120]{0:T(1024)S(1)} %get-tuple-element.6), kind=kOutput, calls=%fused_computation.20 | convolution fusion | flops 16107700224 | bytes 21516288 | tf_op jit(solution)/shard_map/dot_general | solution.py:81
  186.4 0.0 reduce-scatter.3.cloned.1.call-update
  186.4 0.0 copy-start.1
  186.4 0.0 reduce-scatter.5.cloned.1.call-start
  186.4 1.7 fusion.29
  188.2 6.9 %reduce-scatter.3.cloned.1.call-done = bf16[256,512]{1,0:T(8,128)(2,1)} async-done(((bf16[256,1024]{1,0:T(8,128)(2,1)}), bf16[256,512]{1,0:T(8,128)(2,1)}) %reduce-scatter.3.cloned.1.call-update) | async-done | bytes 262160 | tf_op jit(solution)/shard_map/reduce_scatter | solution.py:84
  195.1 2.4 %all_gather.11 = bf16[256,1024]{1,0:T(8,128)(2,1)S(1)} all-gather(bf16[256,512]{1,0:T(8,128)(2,1)} %reduce-scatter.3.cloned.1.call-done), channel_id=1, replica_groups=mesh['band'=16,'ch'=2] {'ch'}, dimensions={1}, use_global_device_ids=true | all-gather | bytes 786432 | tf_op jit(solution)/shard_map/all_gather | solution.py:89
  197.5 0.0 copy-done.4
  197.5 2.9 %convolution_convert_fusion = bf16[256,1024]{1,0:T(8,128)(2,1)} fusion(bf16[512,1024]{1,0:T(8,128)(2,1)S(1)} %copy-done.4, f32[256,512]{1,0:T(8,128)S(1)} %fusion.29, bf16[256,1024]{1,0:T(8,128)(2,1)S(1)} %all_gather.11, bf16[2,1024,512]{2,1,0:T(8,128)(2,1)} %param.22), kind=kOutput, calls=%fused_computation.21 | convolution fusion | flops 537919488 | bytes 3670016 | tf_op jit(solution)/shard_map/dot_general | solution.py:94
  200.4 0.0 reduce-scatter.5.cloned.1.call-update
  200.4 9.2 %reduce-scatter.5.cloned.1.call-done = bf16[256,512]{1,0:T(8,128)(2,1)} async-done(((bf16[256,1024]{1,0:T(8,128)(2,1)}), bf16[256,512]{1,0:T(8,128)(2,1)}) %reduce-scatter.5.cloned.1.call-update) | async-done | bytes 262160 | tf_op jit(solution)/shard_map/reduce_scatter | solution.py:95
  209.7 1.7 add_convert_fusion
  211.4 0.0 copy-done.1
  (4 shorter events, 0.0 us)
Async XLA Ops:
  6.5 153.4 %copy-start = (bf16[512,1024]{1,0:T(8,128)(2,1)S(1)}, bf16[512,1024]{1,0:T(8,128)(2,1)}, u32[]{:S(2)}) copy-start(bf16[512,1024]{1,0:T(8,128)(2,1)} %param.21) | copy-start | bytes 3145732
  6.5 188.6 %reduce-scatter.3.cloned.1.call-start = ((), (), s32[]{:S(2)}) async-start(), calls=%async_computation.2 | async-start | bytes 786432 | tf_op jit(solution)/shard_map/reduce_scatter | solution.py:84
  9.5 45.8 %collective-permute-start.1 = (bf16[50,16384]{1,0:T(8,128)(2,1)S(1)}, bf16[50,16384]{1,0:T(8,128)(2,1)}, u32[]{:S(2)}, u32[]{:S(2)}) collective-permute-start(bf16[50,16384]{1,0:T(8,128)(2,1)S(1)} %dynamic-slice_select_fusion), channel_id=1, source_target_pairs={{2,0},{4,2},{6,4},{8,6},{10,8},{12,10},{14,12},{16,14},{18,16},{20... | collective-permute-start | bytes 4915208 | tf_op jit(solution)/shard_map/ppermute | solution.py:15
  10.8 83.9 %collective-permute-start = (bf16[50,16384]{1,0:T(8,128)(2,1)S(1)}, bf16[50,16384]{1,0:T(8,128)(2,1)}, u32[]{:S(2)}, u32[]{:S(2)}) collective-permute-start(bf16[50,16384]{1,0:T(8,128)(2,1)S(1)} %dynamic-slice_select_fusion), channel_id=1, source_target_pairs={{0,2},{2,4},{4,6},{6,8},{8,10},{10,12},{12,14},{14,16},{16,18},{18... | collective-permute-start | bytes 4915208 | tf_op jit(solution)/shard_map/ppermute | solution.py:12
  99.2 2.2 %copy-start.2 = (bf16[1,16,256,512]{3,2,1,0:T(8,128)(2,1)S(1)}, bf16[1,16,256,512]{3,2,1,0:T(8,128)(2,1)}, u32[]{:S(2)}) copy-start(bf16[1,16,256,512]{3,2,1,0:T(8,128)(2,1)} %param.16) | copy-start | bytes 12582916
  99.3 5.5 %copy-start.3 = (bf16[100,512]{1,0:T(8,128)(2,1)S(1)}, bf16[100,512]{1,0:T(8,128)(2,1)}, u32[]{:S(2)}) copy-start(bf16[100,512]{1,0:T(8,128)(2,1)} %param.17) | copy-start | bytes 307204
  108.8 29.6 %collective-permute-start.3 = (bf16[256,512]{1,0:T(8,128)(2,1)S(1)}, bf16[256,512]{1,0:T(8,128)(2,1)S(1)}, u32[]{:S(2)}, u32[]{:S(2)}) collective-permute-start(bf16[256,512]{1,0:T(8,128)(2,1)S(1)} %convolution_convert_fusion.2), channel_id=1, source_target_pairs={{2,0},{4,2},{6,4},{8,6},{10,8},{12,10},{14,12},{16,14},{18,16},{20... | collective-permute-start | bytes 786440 | tf_op jit(solution)/shard_map/ppermute | solution.py:15
  110.1 28.3 %collective-permute-start.2 = (bf16[256,512]{1,0:T(8,128)(2,1)S(1)}, bf16[256,512]{1,0:T(8,128)(2,1)S(1)}, u32[]{:S(2)}, u32[]{:S(2)}) collective-permute-start(bf16[256,512]{1,0:T(8,128)(2,1)S(1)} %convolution_convert_fusion.2), channel_id=1, source_target_pairs={{0,2},{2,4},{4,6},{6,8},{8,10},{10,12},{12,14},{14,16},{16,18},{18... | collective-permute-start | bytes 786440 | tf_op jit(solution)/shard_map/ppermute | solution.py:12
  172.3 25.2 %copy-start.4 = (bf16[512,1024]{1,0:T(8,128)(2,1)S(1)}, bf16[512,1024]{1,0:T(8,128)(2,1)}, u32[]{:S(2)}) copy-start(bf16[512,1024]{1,0:T(8,128)(2,1)} %param.23) | copy-start | bytes 3145732
  186.4 25.0 %copy-start.1 = (bf16[512,1024]{1,0:T(8,128)(2,1)S(1)}, bf16[512,1024]{1,0:T(8,128)(2,1)}, u32[]{:S(2)}) copy-start(bf16[512,1024]{1,0:T(8,128)(2,1)} %param.21) | copy-start | bytes 3145732
  186.4 23.3 %reduce-scatter.5.cloned.1.call-start = ((), (), s32[]{:S(2)}) async-start(), calls=%async_computation.3 | async-start | bytes 786432 | tf_op jit(solution)/shard_map/reduce_scatter | solution.py:95
Sparse Core Ops, SparseCore 0:
  186.5 8.5 reduce-scatter.2
  200.6 9.0 reduce-scatter.4
where the time goes:
time: 219 us; the launch traced here: 218 us
  waiting for transfers between devices  90.5 us (41%)
  local copies, waits for them, and re-layouts  46.5 us (21%)
  matrix products  36.8 us (17%)
  between operations  15 us (7%)
  starting transfers between devices  14.5 us (7%)
  other arithmetic  8.56 us (4%)
  blocking collectives  6.41 us (3%)
    ppermute x2, waiting for transfers between devices, extended_2(): lax.ppermute(lax.slice_in_dim(block, block.shape[dim] - width, None, axis...  39.4 us
    ppermute x2, waiting for transfers between devices, extended_2(): lax.ppermute(lax.slice_in_dim(block, 0, width, axis=dim), axis, backward)  34.9 us
    gather x1, local copies, waits for them, and re-layouts, on_device(): jnp.take(source_ext, src_local, axis=0).astype(jnp.float32)  21.5 us
    gather x1, local copies, waits for them, and re-layouts, on_device(): jnp.take(target_proj, dst_local, axis=0).astype(jnp.float32)  21.5 us
    dot_general x1, matrix products, on_device(): jnp.dot(onehot, messages, preferred_element_type=jnp.float32, precision=l...  14 us
    dot_general x1, matrix products, on_device(): jnp.dot(edge_hidden, edge_out_weight, preferred_element_type=jnp.float32)  12.4 us
    ppermute x2, starting transfers between devices, extended_2(): lax.ppermute(lax.slice_in_dim(block, block.shape[dim] - width, None, axis...  11.9 us
    reduce_scatter x1, waiting for transfers between devices, on_device(): lax.psum_scatter(partial_out.astype(jnp.bfloat16), 'ch', scatter_dimensio...  9.23 us
  transfers between devices with their start and end apart: 6, of which 4 were waited for; matrix products, arithmetic and copies ran while one was open for 12% of the time, Pallas kernels for 0%

commit v1 on v0

v1 whole, which is shorter than its diff:
```python
import functools

import jax
import jax.numpy as jnp
from jax import lax
from jax.experimental import pallas as pl
from jax.experimental.pallas import tpu as pltpu
from jax.sharding import PartitionSpec as P

MESH = pl.DeviceIdType.MESH
F32 = jnp.float32
BF16 = jnp.bfloat16
VMEM = pl.BlockSpec(memory_space=pltpu.VMEM)
SMEM = pl.BlockSpec(memory_space=pltpu.SMEM)
ANY = pl.BlockSpec(memory_space=pl.ANY)
LIMIT = 60 * 1024 * 1024


def buckets(most):
    pairs = [(3, 5), (4, 6), (5, 6), (5, 7), (6, 8), (8, 10)]
    return [p for p in pairs if max(p) < most] + [(most, most)]


def pack_kernel(half, width, need_ref, rank_ref, grid_ref, out_ref, sem):
    core = lax.axis_index("ch")

    def copy(side, i):
        block = half + i if side == 0 else i
        start = pl.multiple_of((block * 2 + core) * width, width)
        slot = rank_ref[side, i]
        return pltpu.make_async_copy(
            grid_ref.at[:, pl.ds(start, width)], out_ref.at[side, slot], sem.at[side, i]
        )

    for start in (True, False):
        for side in range(2):
            for i in range(half):
                @pl.when(need_ref[side, i] > 0)
                def _():
                    if start:
                        copy(side, i).start()
                    else:
                        copy(side, i).wait()


def exchange_kernel(n, low, high, pk, emb, eo, rv, emb_o, eo_o, send, recv):
    b = lax.axis_index("band")
    c = lax.axis_index("ch")
    up, down = jnp.minimum(b + 1, n - 1), jnp.maximum(b - 1, 0)
    has_up, has_down = b < n - 1, b > 0
    barrier = pltpu.get_barrier_semaphore()
    pl.semaphore_signal(barrier, inc=1, device_id=(b, 1 - c), device_id_type=MESH)

    @pl.when(has_up)
    def _():
        pl.semaphore_signal(barrier, inc=1, device_id=(up, c), device_id_type=MESH)

    @pl.when(has_down)
    def _():
        pl.semaphore_signal(barrier, inc=1, device_id=(down, c), device_id_type=MESH)

    pl.semaphore_wait(barrier, 1 + has_up.astype(jnp.int32) + has_down.astype(jnp.int32))

    def remote(src, dst, k, target):
        return pltpu.make_async_remote_copy(
            src_ref=src, dst_ref=dst, send_sem=send.at[k], recv_sem=recv.at[k],
            device_id=target, device_id_type=MESH,
        )

    fwd = remote(pk.at[0, pl.ds(0, low)], rv.at[0, pl.ds(0, low)], 0, (up, c))
    bwd = remote(pk.at[1, pl.ds(0, high)], rv.at[1, pl.ds(0, high)], 1, (down, c))
    own = [remote(emb, emb_o, 2, (b, 1 - c)), remote(eo, eo_o, 3, (b, 1 - c))]

    @pl.when(has_up)
    def _():
        fwd.start()

    @pl.when(has_down)
    def _():
        bwd.start()

    for one in own:
        one.start()
    for one in own:
        one.wait()

    @pl.when(has_up)
    def _():
        fwd.wait_send()
        bwd.wait_recv()

    @pl.when(has_down)
    def _():
        bwd.wait_send()
        fwd.wait_recv()


def remap_kernel(slots, width, kind_ref, index_ref, limit_ref, grid_ref, rv_ref, w_ref, out_ref, blk, wts, bsem, wsem):
    core = lax.axis_index("ch")
    off = pl.multiple_of(core * width, width)
    for k in range(slots):
        pltpu.make_async_copy(w_ref.at[k, :, pl.ds(off, width)], wts.at[k], wsem.at[k]).start()
    for k in range(slots):
        kind, index = kind_ref[k], index_ref[k]

        @pl.when(kind == 0)
        def _():
            start = pl.multiple_of((index * 2 + core) * width, width)
            pltpu.make_async_copy(grid_ref.at[:, pl.ds(start, width)], blk.at[k], bsem.at[k]).start()

        @pl.when(kind == 1)
        def _():
            pltpu.make_async_copy(rv_ref.at[0, index], blk.at[k], bsem.at[k]).start()

        @pl.when(kind == 2)
        def _():
            pltpu.make_async_copy(rv_ref.at[1, index], blk.at[k], bsem.at[k]).start()

    column = lax.broadcasted_iota(jnp.int32, blk.shape[1:], 1) + core * width
    total = jnp.zeros(out_ref.shape, F32)
    for k in range(slots):
        pltpu.make_async_copy(rv_ref.at[0, 0], blk.at[k], bsem.at[k]).wait()
        pltpu.make_async_copy(w_ref.at[k, :, pl.ds(off, width)], wts.at[k], wsem.at[k]).wait()
        block = blk[k]
        block = jnp.where(column < limit_ref[k], block, jnp.zeros_like(block))
        total += lax.dot_general(wts[k], block, (((1,), (1,)), ((), ())), preferred_element_type=F32)
    out_ref[...] = total


def share_kernel(n, part, out, other, ext, send, recv):
    b = lax.axis_index("band")
    c = lax.axis_index("ch")
    up, down = jnp.minimum(b + 1, n - 1), jnp.maximum(b - 1, 0)
    has_up, has_down = b < n - 1, b > 0
    barrier = pltpu.get_barrier_semaphore()
    pl.semaphore_signal(barrier, inc=1, device_id=(b, 1 - c), device_id_type=MESH)

    @pl.when(has_up)
    def _():
        pl.semaphore_signal(barrier, inc=1, device_id=(up, c), device_id_type=MESH)

    @pl.when(has_down)
    def _():
        pl.semaphore_signal(barrier, inc=1, device_id=(down, c), device_id_type=MESH)

    pl.semaphore_wait(barrier, 1 + has_up.astype(jnp.int32) + has_down.astype(jnp.int32))

    def remote(src, dst, k, target):
        return pltpu.make_async_remote_copy(
            src_ref=src, dst_ref=dst, send_sem=send.at[k], recv_sem=recv.at[k],
            device_id=target, device_id_type=MESH,
        )

    swap = remote(part, other, 0, (b, 1 - c))
    swap.start()
    swap.wait()
    ext[1] = (part[...] + other[...]).astype(BF16)
    fwd = remote(ext.at[1], ext.at[0], 1, (up, c))
    bwd = remote(ext.at[1], ext.at[2], 2, (down, c))

    @pl.when(has_up)
    def _():
        fwd.start()

    @pl.when(has_down)
    def _():
        bwd.start()

    @pl.when(has_up)
    def _():
        fwd.wait_send()
        bwd.wait_recv()

    @pl.when(has_down)
    def _():
        bwd.wait_send()
        fwd.wait_recv()

    out[...] = ext[...]

    @pl.when(b == 0)
    def _():
        out[0] = jnp.zeros(out.shape[1:], BF16)

    @pl.when(b == n - 1)
    def _():
        out[2] = jnp.zeros(out.shape[1:], BF16)


def silu(v):
    return (0.5 * v) * (1.0 + jnp.tanh(0.5 * v))


def edge_kernel(chunk, ext, emb, emb_o, src, dst, win, agg_out, init_out, init_s, table, acc):
    b = lax.axis_index("band")
    c = lax.axis_index("ch")
    nodes = ext.shape[1]
    half = emb.shape[1]
    rem = ext[...].reshape(3 * nodes, ext.shape[2])
    mine = pl.ds(pl.multiple_of(c * half, half), half)
    theirs = pl.ds(pl.multiple_of((1 - c) * half, half), half)
    init_s[:, mine] = jnp.dot(rem, emb[...], preferred_element_type=F32).astype(BF16)
    init_s[:, theirs] = jnp.dot(rem, emb_o[...], preferred_element_type=F32).astype(BF16)
    init_out[...] = init_s[nodes:2 * nodes, :]
    source = jnp.dot(init_s[...], win[0], preferred_element_type=F32)
    table[:, :3 * nodes] = source.T.astype(BF16)
    target = jnp.dot(init_s[nodes:2 * nodes, :], win[1], preferred_element_type=F32)
    table[:, 3 * nodes:] = target.T.astype(BF16)
    acc[...] = jnp.zeros_like(acc)
    one, zero = jnp.ones((), BF16), jnp.zeros((), BF16)

    def step(i, carry):
        cols = pl.ds(pl.multiple_of(i * chunk, chunk), chunk)
        s = src[:, cols] - (b - 1) * nodes
        d = dst[:, cols] - b * nodes
        from_src = lax.broadcasted_iota(jnp.int32, (3 * nodes, chunk), 0) == s
        from_dst = lax.broadcasted_iota(jnp.int32, (nodes, chunk), 0) == d
        hot_src = jnp.where(from_src, 1.0, 0.0).astype(BF16)
        hot_dst = jnp.where(from_dst, 1.0, 0.0).astype(BF16)
        pre = jnp.dot(table[...], jnp.concatenate([hot_src, hot_dst], axis=0), preferred_element_type=F32)
        hidden = silu(pre).astype(BF16)
        acc[...] += lax.dot_general(hot_dst, hidden, (((1,), (1,)), ((), ())), preferred_element_type=F32)
        return carry

    lax.fori_loop(0, src.shape[1] // chunk, step, 0)
    agg_out[...] = acc[...].astype(BF16)


def node_kernel(agg, init, eo, eo_o, nin, nout, out, agg_o, give, take, send, recv):
    b = lax.axis_index("band")
    c = lax.axis_index("ch")
    half = nin.shape[2]
    barrier = pltpu.get_barrier_semaphore()
    pl.semaphore_signal(barrier, inc=1, device_id=(b, 1 - c), device_id_type=MESH)
    pl.semaphore_wait(barrier, 1)

    def remote(src, dst, k):
        return pltpu.make_async_remote_copy(
            src_ref=src, dst_ref=dst, send_sem=send.at[k], recv_sem=recv.at[k],
            device_id=(b, 1 - c), device_id_type=MESH,
        )

    swap = remote(agg, agg_o, 0)
    swap.start()
    direct = jnp.dot(init[...], nin[0], preferred_element_type=F32)
    own = jnp.dot(agg[...], eo[...], preferred_element_type=F32)
    swap.wait()
    total = (own + jnp.dot(agg_o[...], eo_o[...], preferred_element_type=F32)).astype(BF16)
    update = silu(direct + jnp.dot(total, nin[1], preferred_element_type=F32)).astype(BF16)
    mine = pl.ds(pl.multiple_of(c * half, half), half)
    theirs = pl.ds(pl.multiple_of((1 - c) * half, half), half)
    give[...] = jnp.dot(update, nout[:, theirs], preferred_element_type=F32).astype(BF16)
    last = remote(give, take, 1)
    last.start()
    kept = init[:, mine].astype(F32) + jnp.dot(update, nout[:, mine], preferred_element_type=F32)
    last.wait()
    out[...] = (kept + take[...].astype(F32)).astype(BF16)


def on_device(
    grid_field, band_points, block_ids, block_count, block_weight, embed_weight,
    edge_src, edge_dst, edge_in_weight, edge_out_weight, node_in_weight, node_out_weight,
):
    n = lax.axis_size("band")
    b = lax.axis_index("band")
    channels, points = grid_field.shape
    slots, nodes, block_len = block_weight.shape[1:]
    sub = points // block_len
    half = sub // 2
    width = block_len // 2
    hid = embed_weight.shape[1]
    params = functools.partial(pltpu.CompilerParams, vmem_limit_bytes=LIMIT)

    meta = jnp.concatenate([block_ids[0], block_count, band_points])
    meta = lax.all_gather(meta, "band", axis=0)
    ids, count, live = meta[:, :slots], meta[:, slots], meta[:, slots + 1]
    bands = lax.iota(jnp.int32, n)
    rel = ids - bands[:, None] * sub + half
    used = lax.broadcasted_iota(jnp.int32, (n, slots), 1) < count[:, None]
    cand = lax.iota(jnp.int32, 2 * half)
    spot = jnp.where(cand < half, cand, cand + sub)
    below = jnp.concatenate([live[:1], live[:-1]])
    above = jnp.concatenate([live[1:], live[-1:]])
    start = jnp.where(cand < half, cand + half, cand - half) * block_len
    alive = jnp.where(cand[None] < half, start[None] < below[:, None], start[None] < above[:, None])
    named = jnp.any((rel[:, :, None] == spot[None, None, :]) & used[:, :, None], axis=1)
    need = (named & alive).astype(jnp.int32).reshape(n, 2, half)
    order = lax.iota(jnp.int32, half)
    rank = jnp.sum(jnp.where(order[None, :] < order[:, None], need[:, :, None, :], 0), axis=3)
    most = jnp.max(jnp.sum(need, axis=2), axis=0)
    sizes = buckets(half)
    choice = jnp.int32(0)
    for low, high in sizes[:-1]:
        choice += ((most[0] > low) | (most[1] > high)).astype(jnp.int32)

    up, down = jnp.minimum(b + 1, n - 1), jnp.maximum(b - 1, 0)
    pick = lambda a: jnp.stack([
        jnp.where(b < n - 1, lax.dynamic_index_in_dim(a, up, 0, False)[0], 0),
        jnp.where(b > 0, lax.dynamic_index_in_dim(a, down, 0, False)[1], 0),
    ])
    send_need, send_rank = pick(need), pick(rank)

    slot_shape = (2, half, channels, width)
    packed = pl.pallas_call(
        functools.partial(pack_kernel, half, width),
        out_shape=jax.ShapeDtypeStruct(slot_shape, BF16),
        in_specs=[SMEM, SMEM, ANY], out_specs=VMEM,
        scratch_shapes=[pltpu.SemaphoreType.DMA((2, half))],
        compiler_params=params(),
    )(send_need, send_rank, grid_field)

    def exchange(i, low, high, *args):
        return pl.pallas_call(
            functools.partial(exchange_kernel, n, low, high),
            out_shape=(
                jax.ShapeDtypeStruct(slot_shape, BF16),
                jax.ShapeDtypeStruct(embed_weight.shape, BF16),
                jax.ShapeDtypeStruct(edge_out_weight.shape, BF16),
            ),
            in_specs=[ANY] * 3, out_specs=(ANY,) * 3,
            scratch_shapes=[pltpu.SemaphoreType.DMA((4,)), pltpu.SemaphoreType.DMA((4,))],
            compiler_params=params(collective_id=i, has_side_effects=True),
        )(*args)

    received, embed_other, eo_other = lax.switch(
        choice,
        [functools.partial(exchange, i, low, high) for i, (low, high) in enumerate(sizes)],
        packed, embed_weight, edge_out_weight,
    )

    mine = lax.dynamic_index_in_dim(rel, b, 0, False)
    my_rank = lax.dynamic_index_in_dim(rank, b, 0, False)
    my_need = lax.dynamic_index_in_dim(need, b, 0, False)
    live_slot = lax.iota(jnp.int32, slots) < block_count[0]
    is_low, is_high = mine < half, mine >= half + sub
    side = jnp.where(is_low, mine, mine - sub)
    hit = side[:, None] == cand[None]
    far_index = jnp.sum(jnp.where(hit, my_rank.reshape(1, -1), 0), axis=1)
    far_need = jnp.sum(jnp.where(hit, my_need.reshape(1, -1), 0), axis=1) > 0
    far = (is_low | is_high) & far_need & live_slot
    kind = jnp.where(far, jnp.where(is_low, 1, 2), 0).astype(jnp.int32)
    local = jnp.clip(mine - half, 0, sub - 1)
    index = jnp.where(far, far_index, local).astype(jnp.int32)
    owner_live = jnp.where(is_low, live[down], jnp.where(is_high, live[up], band_points[0]))
    inner = jnp.where(is_low, mine + half, jnp.where(is_high, mine - half - sub, mine - half))
    limit = jnp.clip(owner_live - inner * block_len, 0, block_len)
    reachable = live_slot & (far | ~(is_low | is_high))
    limit = jnp.where(reachable, limit, 0).astype(jnp.int32)

    part = pl.pallas_call(
        functools.partial(remap_kernel, slots, width),
        out_shape=jax.ShapeDtypeStruct((nodes, channels), F32),
        in_specs=[SMEM, SMEM, SMEM, ANY, ANY, ANY], out_specs=VMEM,
        scratch_shapes=[
            pltpu.VMEM((slots, channels, width), BF16),
            pltpu.VMEM((slots, nodes, width), BF16),
            pltpu.SemaphoreType.DMA((slots,)),
            pltpu.SemaphoreType.DMA((slots,)),
        ],
        compiler_params=params(),
    )(kind, index, limit, grid_field, received, block_weight[0])

    ext = pl.pallas_call(
        functools.partial(share_kernel, n),
        out_shape=jax.ShapeDtypeStruct((3, nodes, channels), BF16),
        in_specs=[VMEM], out_specs=VMEM,
        scratch_shapes=[
            pltpu.VMEM((nodes, channels), F32),
            pltpu.VMEM((3, nodes, channels), BF16),
            pltpu.SemaphoreType.DMA((3,)), pltpu.SemaphoreType.DMA((3,)),
        ],
        compiler_params=params(collective_id=len(sizes), has_side_effects=True),
    )(part)

    edges = edge_src.shape[0]
    chunk = max(c for c in (512, 256, 128) if edges % c == 0)
    agg, initial = pl.pallas_call(
        functools.partial(edge_kernel, chunk),
        out_shape=(
            jax.ShapeDtypeStruct((nodes, hid), BF16),
            jax.ShapeDtypeStruct((nodes, 2 * hid), BF16),
        ),
        in_specs=[VMEM] * 6, out_specs=(VMEM, VMEM),
        scratch_shapes=[
            pltpu.VMEM((3 * nodes, 2 * hid), BF16),
            pltpu.VMEM((hid, 4 * nodes), BF16),
            pltpu.VMEM((nodes, hid), F32),
        ],
        compiler_params=params(),
    )(ext, embed_weight, embed_other, edge_src.reshape(1, -1), edge_dst.reshape(1, -1), edge_in_weight)

    return pl.pallas_call(
        node_kernel,
        out_shape=jax.ShapeDtypeStruct((nodes, hid), BF16),
        in_specs=[VMEM] * 6, out_specs=VMEM,
        scratch_shapes=[
            pltpu.VMEM((nodes, hid), BF16),
            pltpu.VMEM((nodes, hid), BF16),
            pltpu.VMEM((nodes, hid), BF16),
            pltpu.SemaphoreType.DMA((2,)), pltpu.SemaphoreType.DMA((2,)),
        ],
        compiler_params=params(collective_id=len(sizes) + 1, has_side_effects=True),
    )(agg, initial, edge_out_weight, eo_other, node_in_weight, node_out_weight)


def solution(mesh):
    return jax.shard_map(
        on_device,
        mesh=mesh,
        in_specs=(
            P(None, "band"), P("band"), P("band", None), P("band"),
            P("band", None, None, None), P(None, "ch"), P("band"), P("band"),
            P(None, None, "ch"), P("ch", None), P(None, None, "ch"), P("ch", None),
        ),
        out_specs=P("band", "ch"),
        check_vma=False,
    )
```

time: 219 us -> 90.5 us (0.41)
  waiting for transfers between devices: 90.5 us -> 0 us
  Pallas kernels: 0 us -> 52.9 us
  local copies, waits for them, and re-layouts: 46.5 us -> 5.6 us
  matrix products: 36.8 us -> 0 us
  starting transfers between devices: 14.5 us -> 0 us
  blocking collectives: 6.41 us -> 16.2 us
  between operations: 15 us -> 8.84 us
    ppermute x4 -> x0, waiting for transfers between devices: 74.3 us -> none  [the longest x2 39.4 us: extended_2(): lax.ppermute(lax.slice_in_dim(block, block.shape[dim] - width, None, axis...]
    pallas_call x0 -> x6, Pallas kernels: none -> 52.9 us  [the longest x1 15.6 us: exchange(): pl.pallas_call(functools.partial(exchange_kernel, n, low, high), out_shap...]
    gather x2 -> x0, local copies, waits for them, and re-layouts: 42.9 us -> none  [the longest x1 21.5 us: on_device(): jnp.take(source_ext, src_local, axis=0).astype(jnp.float32)]
    dot_general x9 -> x0, matrix products: 36.8 us -> none  [the longest x1 14 us: on_device(): jnp.dot(onehot, messages, preferred_element_type=jnp.float32, precision=l...]
    unnamed x0 -> x1, blocking collectives: none -> 16.2 us
    reduce_scatter x2 -> x0, waiting for transfers between devices: 16.2 us -> none  [the longest x1 9.23 us: on_device(): lax.psum_scatter(partial_out.astype(jnp.bfloat16), 'ch', scatter_dimensio...]
    ppermute x4 -> x0, starting transfers between devices: 14.5 us -> none  [the longest x2 11.9 us: extended_2(): lax.ppermute(lax.slice_in_dim(block, block.shape[dim] - width, None, axis...]
    all_gather x3 -> x0, blocking collectives: 6.41 us -> none  [the longest x1 2.38 us: on_device(): lax.all_gather(agg_half, 'ch', axis=1, tiled=True)]
  transfers between devices with their start and end apart: 6 -> 0, of which waited for: 4 -> 0; matrix products, arithmetic and copies ran while one was open for 12% -> 0% of each run, Pallas kernels for 0% -> 0%
where the time goes in v1:
time: 90.5 us; the launch traced here: 90.6 us
  Pallas kernels  52.9 us (58%)
  blocking collectives  16.2 us (18%)
  between operations  8.84 us (10%)
  other arithmetic  6.96 us (8%)
  local copies, waits for them, and re-layouts  5.6 us (6%)
    unnamed x1, blocking collectives  16.2 us
    pallas_call x1, Pallas kernels, exchange(): pl.pallas_call(functools.partial(exchange_kernel, n, low, high), out_shap...  15.6 us
    pallas_call x1, Pallas kernels, on_device(): pl.pallas_call(functools.partial(edge_kernel, chunk), out_shape=(jax.Shap...  14.7 us
    pallas_call x1, Pallas kernels, on_device(): pl.pallas_call(functools.partial(share_kernel, n), out_shape=jax.ShapeDty...  8.81 us
    pallas_call x1, Pallas kernels, on_device(): pl.pallas_call(node_kernel, out_shape=jax.ShapeDtypeStruct((nodes, hid),...  7.08 us
    pallas_call x1, Pallas kernels, on_device(): pl.pallas_call(functools.partial(remap_kernel, slots, width), out_shape=j...  4.73 us
    unnamed x9, local copies, waits for them, and re-layouts  2.93 us
    pallas_call x1, Pallas kernels, on_device(): pl.pallas_call(functools.partial(pack_kernel, half, width), out_shape=jax...  2.05 us

profile of v1, /device:TPU:0, one launch (start us, length us, event | category | flops | bytes accessed | tf_op | source)
XLA Modules:
  0.0 90.6 jit_solution(12632214702152191463)
XLA Ops:
  1.3 1.2 %dynamic-slice.2 = u32[1]{0:T(128)} dynamic-slice(u32[32]{0:T(128)} %constant.105, u32[]{:T(128)S(6)} %add.102), dynamic_slice_sizes={1} | dynamic-slice | bytes 12
  3.3 0.8 add_dynamic-update-slice_fusion
  4.1 16.2 %all-reduce = s32[288]{0:T(512)S(1)} all-reduce(s32[288]{0:T(512)S(1)} %add_dynamic-update-slice_fusion), channel_id=2, replica_groups=mesh['band'=16,'ch'=2] {'band'}, use_global_device_ids=true, to_apply=%add | all-reduce | flops 288 | bytes 2304
  20.3 0.1 reshape.255
  20.4 0.2 slice_reduce_fusion.1
  20.6 0.7 fusion.10
  21.2 0.7 pad_add_fusion.2
  21.9 0.8 pad_add_fusion.3
  22.7 0.1 fusion
  22.8 0.2 slice_reduce_fusion.2
  23.0 0.6 constant_dynamic-slice_fusion.5
  23.6 0.1 iota_compare_fusion.1
  23.6 0.2 and_reduce_fusion
  23.8 0.1 copy.17
  23.9 0.1 copy.18
  24.0 0.4 fusion.8
  24.4 0.6 fusion.11
  31.8 0.6 select_reduce_fusion
  32.5 0.6 pad_add_fusion
  33.1 0.1 broadcast_in_dim.89
  33.2 0.1 broadcast_in_dim.97
  33.3 0.2 select_reduce_fusion.1
  33.4 1.8 %and_select_fusion = (s32[16]{0:T(128)}, pred[16]{0:T(512)(128)(4,1)S(1)}) fusion(s32[16]{0:T(128)S(1)} %get-tuple-element.87, s32[]{:T(128)} %bitcast.24, s32[]{:T(128)} %bitcast.8, s32[]{:T(128)} %bitcast.7, s32[]{:T(128)} %bitcast.25, s32[16]{0:T(128)S(1)} %get-tuple-element.81), kind=kLoop, calls=%fused_computation.23 | loop fusion | flops 336 | bytes 224 | tf_op jit(solution)/shard_map/jit(_where)/select_n | solution.py:348
  35.3 0.6 clamp_select_fusion
  35.9 0.0 copy-start
  35.9 0.0 copy-start.1
  35.9 2.1 %shard_map.118 = bf16[2,16,100,256]{3,2,1,0:T(8,128)(2,1)S(1)} custom-call(s32[2,16]{1,0:T(2,128)} %get-tuple-element.104.need_ref, s32[2,16]{1,0:T(2,128)} %get-tuple-element.105.rank_ref, bf16[100,16384]{1,0:T(8,128)(2,1)} %grid_ref.3), custom_call_target="tpu_custom_call" | custom-call | tf_op jit(solution)/shard_map/pallas_call | solution.py:304
  37.9 0.0 copy-done
  37.9 0.0 copy-done.1
  37.9 15.6 %conditional.1 = ((bf16[2,16,100,256]{3,2,1,0:T(8,128)(2,1)}, bf16[100,512]{1,0:T(8,128)(2,1)S(1)}, bf16[512,1024]{1,0:T(8,128)(2,1)})) conditional(s32[]{:T(128)} %bitcast.10, (bf16[2,16,100,256]{3,2,1,0:T(8,128)(2,1)S(1)}, bf16[100,512]{1,0:T(8,128)(2,1)S(1)}, bf16[512,1024]{1,0:T(8,128)(2,1)S(1)}) %tuple.63, ...), branch_computations={%region_6.7_spmd, %region_7.8_spmd, %region_8.9_spmd, %region_9.10... | conditional | bytes 8 | solution.py:325
  38.0 15.6 %branch_2_fun.1 = (bf16[2,16,100,256]{3,2,1,0:T(8,128)(2,1)}, bf16[100,512]{1,0:T(8,128)(2,1)S(1)}, bf16[512,1024]{1,0:T(8,128)(2,1)}) custom-call(bf16[2,16,100,256]{3,2,1,0:T(8,128)(2,1)S(1)} %get-tuple-element.53.pk, bf16[100,512]{1,0:T(8,128)(2,1)S(1)} %get-tuple-element.54.emb, bf16[512,1024]{1,0:T(8,128)(2,1)S(1)} %get-tuple-element.55.eo), custom_call_target="tpu_custom_call" | custom-call | tf_op jit(solution)/shard_map/cond/branch_2_fun/pallas_call | solution.py:313
  53.6 4.7 %shard_map.119.part = f32[256,100]{1,0:T(8,128)} custom-call(s32[16]{0:T(128)} %get-tuple-element.101.kind_ref, s32[16]{0:T(128)} %get-tuple-element.100.index_ref, s32[16]{0:T(128)} %get-tuple-element.84.limit_ref, bf16[100,16384]{1,0:T(8,128)(2,1)} %grid_ref.3, bf16[2,16,100,256]{3,2,1,0:T(8,128)(2,1)} %get-tuple-element.73.rv_ref, ...), custom_call_target="tpu_custom_call" | custom-call | tf_op jit(solution)/shard_map/pallas_call | solution.py:350
  58.3 0.0 copy-start.2
  58.3 8.8 %shard_map.120.ext = bf16[3,256,100]{2,1,0:T(8,128)(2,1)} custom-call(f32[256,100]{1,0:T(8,128)} %shard_map.119.part), custom_call_target="tpu_custom_call" | custom-call | tf_op jit(solution)/shard_map/pallas_call | solution.py:363
  67.2 14.7 %shard_map.121 = (bf16[256,512]{1,0:T(8,128)(2,1)}, bf16[256,1024]{1,0:T(8,128)(2,1)}) custom-call(bf16[3,256,100]{2,1,0:T(8,128)(2,1)} %shard_map.120.ext, bf16[100,512]{1,0:T(8,128)(2,1)S(1)} %copy-done.1, bf16[100,512]{1,0:T(8,128)(2,1)S(1)} %get-tuple-element.74.emb_o, s32[1,5120]{1,0:T(1,128)} %bitcast.27, s32[1,5120]{1,0:T(1,128)} %bitcast.28, ...), custom_call_target="tpu_custom_call" | custom-call | tf_op jit(solution)/shard_map/pallas_call | solution.py:377
  81.8 0.0 copy-done.2
  81.8 7.1 %shard_map.122 = bf16[256,512]{1,0:T(8,128)(2,1)} custom-call(bf16[256,512]{1,0:T(8,128)(2,1)} %get-tuple-element.75.agg, bf16[256,1024]{1,0:T(8,128)(2,1)} %get-tuple-element.76.init, bf16[512,1024]{1,0:T(8,128)(2,1)S(1)} %copy-done, bf16[512,1024]{1,0:T(8,128)(2,1)S(1)} %copy-done.2, bf16[2,1024,512]{2,1,0:T(8,128)(2,1)} %nin.1, bf16[512,1024]{1,0:T(8,128)(2,1)} %nout.1), custom_call_target="tpu_custom_call" | custom-call | tf_op jit(solution)/shard_map/pallas_call | solution.py:392
  88.9 1.7 %copy.49 = bf16[256,512]{1,0:T(8,128)(2,1)} copy(bf16[256,512]{1,0:T(8,128)(2,1)} %shard_map.122) | data formatting | bytes 524288
  (14 shorter events, 0.1 us)
Async XLA Ops:
  35.9 2.1 %copy-start = (bf16[512,1024]{1,0:T(8,128)(2,1)S(1)}, bf16[512,1024]{1,0:T(8,128)(2,1)}, u32[]{:S(2)}) copy-start(bf16[512,1024]{1,0:T(8,128)(2,1)} %eo.1) | copy-start | bytes 3145732
  35.9 2.1 %copy-start.1 = (bf16[100,512]{1,0:T(8,128)(2,1)S(1)}, bf16[100,512]{1,0:T(8,128)(2,1)}, u32[]{:S(2)}) copy-start(bf16[100,512]{1,0:T(8,128)(2,1)} %emb.1) | copy-start | bytes 307204
  58.3 23.5 %copy-start.2 = (bf16[512,1024]{1,0:T(8,128)(2,1)S(1)}, bf16[512,1024]{1,0:T(8,128)(2,1)}, u32[]{:S(2)}) copy-start(bf16[512,1024]{1,0:T(8,128)(2,1)} %get-tuple-element.77.eo_o) | copy-start | bytes 3145732

commit v2 on v1

--- a/solution.py
+++ b/solution.py
@@ -13,7 +13,8 @@
 VMEM = pl.BlockSpec(memory_space=pltpu.VMEM)
 SMEM = pl.BlockSpec(memory_space=pltpu.SMEM)
 ANY = pl.BlockSpec(memory_space=pl.ANY)
-LIMIT = 60 * 1024 * 1024
+SMALL = 12 * 1024 * 1024
+LARGE = 32 * 1024 * 1024
 
 
 def buckets(most):
@@ -21,26 +22,128 @@
     return [p for p in pairs if max(p) < most] + [(most, most)]
 
 
-def pack_kernel(half, width, need_ref, rank_ref, grid_ref, out_ref, sem):
+def meta_kernel(n, slots, sub, block_len, sizes, ids, count, live, out, choice, row, rows, send, recv):
+    b = lax.axis_index("band")
+    c = lax.axis_index("ch")
+    half = sub // 2
+    row[:, :slots] = ids[...]
+    row[:, slots:2 * slots] = jnp.full((1, slots), count[0], jnp.int32)
+    row[:, 2 * slots:3 * slots] = jnp.full((1, slots), live[0], jnp.int32)
+    row[:, 3 * slots:] = jnp.zeros((1, row.shape[1] - 3 * slots), jnp.int32)
+    barrier = pltpu.get_barrier_semaphore()
+
+    def greet(d, carry):
+        pl.semaphore_signal(barrier, inc=1, device_id=(lax.rem(b + d, n), c), device_id_type=MESH)
+        return carry
+
+    lax.fori_loop(1, n, greet, 0)
+    pl.semaphore_wait(barrier, n - 1)
+
+    def copy(d):
+        return pltpu.make_async_remote_copy(
+            src_ref=row, dst_ref=rows.at[b], send_sem=send.at[d], recv_sem=recv.at[d],
+            device_id=(lax.rem(b + d, n), c), device_id_type=MESH,
+        )
+
+    def begin(d, carry):
+        copy(d).start()
+        return carry
+
+    def arrive(d, carry):
+        pltpu.make_async_remote_copy(
+            src_ref=row, dst_ref=rows.at[lax.rem(b + n - d, n)], send_sem=send.at[d], recv_sem=recv.at[d],
+            device_id=(lax.rem(b + d, n), c), device_id_type=MESH,
+        ).wait()
+        return carry
+
+    lax.fori_loop(1, n, begin, 0)
+    rows[b] = row[...]
+    lax.fori_loop(1, n, arrive, 0)
+    out[...] = rows[...]
+    every = rows[:, 0, :]
+    named, most, points = every[:, :slots], every[:, slots:2 * slots], every[:, 2 * slots:2 * slots + 1]
+    below = jnp.concatenate([points[:1], points[:-1]], axis=0)
+    above = jnp.concatenate([points[1:], points[-1:]], axis=0)
+    bands = lax.broadcasted_iota(jnp.int32, (n, 1), 0)
+    rel = named - bands * sub + half
+    rel = jnp.where(lax.broadcasted_iota(jnp.int32, (n, slots), 1) < most, rel, -1)
+    counts = []
+    for side in range(2):
+        total = jnp.zeros((n, 1), F32)
+        for i in range(half):
+            spot = i if side == 0 else half + sub + i
+            hit = jnp.max(jnp.where(rel == spot, 1.0, 0.0), axis=1, keepdims=True)
+            alive = (half + i) * block_len < below if side == 0 else i * block_len < above
+            total += jnp.where(alive, hit, 0.0)
+        counts.append(jnp.max(total, axis=0, keepdims=True))
+    pick = jnp.zeros((1, 1), jnp.int32)
+    for low, high in sizes[:-1]:
+        pick += jnp.where((counts[0] > low) | (counts[1] > high), 1, 0)
+    choice[...] = jnp.broadcast_to(pick, choice.shape)
+
+
+def pack_kernel(n, slots, sub, block_len, meta, grid_ref, out_ref, kind, index, limit, need, rank, mine, place, sem):
+    b = lax.axis_index("band")
     core = lax.axis_index("ch")
+    half = sub // 2
+    width = block_len // 2
+
+    def mark(side, band, owner, flags, ranks, active):
+        for i in range(half):
+            flags[side, i] = 0
+        for k in range(slots):
+            rel = meta[band, 0, k] - band * sub + half
+            i = rel if side == 0 else rel - half - sub
+            inner = rel + half if side == 0 else i
+            good = (i >= 0) & (i < half) & (k < meta[band, 0, slots])
+            good &= (inner * block_len < meta[owner, 0, 2 * slots]) & active
+            i = jnp.clip(i, 0, half - 1)
+            flags[side, i] = flags[side, i] | good.astype(jnp.int32)
+        run = jnp.int32(0)
+        for i in range(half):
+            ranks[side, i] = run
+            run += flags[side, i]
+
+    up, down = jnp.minimum(b + 1, n - 1), jnp.maximum(b - 1, 0)
 
     def copy(side, i):
         block = half + i if side == 0 else i
         start = pl.multiple_of((block * 2 + core) * width, width)
-        slot = rank_ref[side, i]
         return pltpu.make_async_copy(
-            grid_ref.at[:, pl.ds(start, width)], out_ref.at[side, slot], sem.at[side, i]
+            grid_ref.at[:, pl.ds(start, width)], out_ref.at[side, rank[side, i]], sem.at[side, i]
         )
 
-    for start in (True, False):
-        for side in range(2):
-            for i in range(half):
-                @pl.when(need_ref[side, i] > 0)
-                def _():
-                    if start:
-                        copy(side, i).start()
-                    else:
-                        copy(side, i).wait()
+    def each(begin, side):
+        for i in range(half):
+            @pl.when(need[side, i] > 0)
+            def _():
+                if begin:
+                    copy(side, i).start()
+                else:
+                    copy(side, i).wait()
+
+    mark(0, up, b, need, rank, b < n - 1)
+    each(True, 0)
+    mark(1, down, b, need, rank, b > 0)
+    each(True, 1)
+    mark(0, b, down, mine, place, b > 0)
+    mark(1, b, up, mine, place, b < n - 1)
+    for k in range(slots):
+        rel = meta[b, 0, k] - b * sub + half
+        is_low, is_high = rel < half, rel >= half + sub
+        side = is_high.astype(jnp.int32)
+        i = jnp.clip(jnp.where(is_low, rel, rel - half - sub), 0, half - 1)
+        used = k < meta[b, 0, slots]
+        outside = is_low | is_high
+        far = outside & used & (mine[side, i] > 0)
+        owner = jnp.where(is_low, down, jnp.where(is_high, up, b))
+        inner = jnp.where(is_low, rel + half, jnp.where(is_high, rel - half - sub, rel - half))
+        span = jnp.clip(meta[owner, 0, 2 * slots] - inner * block_len, 0, block_len)
+        kind[k] = jnp.where(far, 1 + side, 0)
+        index[k] = jnp.where(far, place[side, i], jnp.clip(rel - half, 0, sub - 1))
+        limit[k] = jnp.where(used & (far | ~outside), span, 0)
+    each(False, 0)
+    each(False, 1)
 
 
 def exchange_kernel(n, low, high, pk, emb, eo, rv, emb_o, eo_o, send, recv):
@@ -222,7 +325,7 @@
         acc[...] += lax.dot_general(hot_dst, hidden, (((1,), (1,)), ((), ())), preferred_element_type=F32)
         return carry
 
-    lax.fori_loop(0, src.shape[1] // chunk, step, 0)
+    lax.fori_loop(0, src.shape[1] // chunk, step, 0, unroll=True)
     agg_out[...] = acc[...].astype(BF16)
 
 
@@ -262,52 +365,40 @@
     edge_src, edge_dst, edge_in_weight, edge_out_weight, node_in_weight, node_out_weight,
 ):
     n = lax.axis_size("band")
-    b = lax.axis_index("band")
     channels, points = grid_field.shape
     slots, nodes, block_len = block_weight.shape[1:]
     sub = points // block_len
     half = sub // 2
     width = block_len // 2
     hid = embed_weight.shape[1]
-    params = functools.partial(pltpu.CompilerParams, vmem_limit_bytes=LIMIT)
-
-    meta = jnp.concatenate([block_ids[0], block_count, band_points])
-    meta = lax.all_gather(meta, "band", axis=0)
-    ids, count, live = meta[:, :slots], meta[:, slots], meta[:, slots + 1]
-    bands = lax.iota(jnp.int32, n)
-    rel = ids - bands[:, None] * sub + half
-    used = lax.broadcasted_iota(jnp.int32, (n, slots), 1) < count[:, None]
-    cand = lax.iota(jnp.int32, 2 * half)
-    spot = jnp.where(cand < half, cand, cand + sub)
-    below = jnp.concatenate([live[:1], live[:-1]])
-    above = jnp.concatenate([live[1:], live[-1:]])
-    start = jnp.where(cand < half, cand + half, cand - half) * block_len
-    alive = jnp.where(cand[None] < half, start[None] < below[:, None], start[None] < above[:, None])
-    named = jnp.any((rel[:, :, None] == spot[None, None, :]) & used[:, :, None], axis=1)
-    need = (named & alive).astype(jnp.int32).reshape(n, 2, half)
-    order = lax.iota(jnp.int32, half)
-    rank = jnp.sum(jnp.where(order[None, :] < order[:, None], need[:, :, None, :], 0), axis=3)
-    most = jnp.max(jnp.sum(need, axis=2), axis=0)
+    params = lambda limit, **kw: pltpu.CompilerParams(vmem_limit_bytes=limit, **kw)
+
     sizes = buckets(half)
-    choice = jnp.int32(0)
-    for low, high in sizes[:-1]:
-        choice += ((most[0] > low) | (most[1] > high)).astype(jnp.int32)
-
-    up, down = jnp.minimum(b + 1, n - 1), jnp.maximum(b - 1, 0)
-    pick = lambda a: jnp.stack([
-        jnp.where(b < n - 1, lax.dynamic_index_in_dim(a, up, 0, False)[0], 0),
-        jnp.where(b > 0, lax.dynamic_index_in_dim(a, down, 0, False)[1], 0),
-    ])
-    send_need, send_rank = pick(need), pick(rank)
+    meta, choice = pl.pallas_call(
+        functools.partial(meta_kernel, n, slots, sub, block_len, sizes),
+        out_shape=(
+            jax.ShapeDtypeStruct((n, 1, 128), jnp.int32),
+            jax.ShapeDtypeStruct((1, 128), jnp.int32),
+        ),
+        in_specs=[VMEM, SMEM, SMEM], out_specs=(VMEM, VMEM),
+        scratch_shapes=[
+            pltpu.VMEM((1, 128), jnp.int32),
+            pltpu.VMEM((n, 1, 128), jnp.int32),
+            pltpu.SemaphoreType.DMA((n,)), pltpu.SemaphoreType.DMA((n,)),
+        ],
+        compiler_params=params(SMALL, collective_id=len(sizes) + 2, has_side_effects=True),
+    )(block_ids, block_count, band_points)
 
     slot_shape = (2, half, channels, width)
-    packed = pl.pallas_call(
-        functools.partial(pack_kernel, half, width),
-        out_shape=jax.ShapeDtypeStruct(slot_shape, BF16),
-        in_specs=[SMEM, SMEM, ANY], out_specs=VMEM,
-        scratch_shapes=[pltpu.SemaphoreType.DMA((2, half))],
-        compiler_params=params(),
-    )(send_need, send_rank, grid_field)
+    lists = jax.ShapeDtypeStruct((slots,), jnp.int32)
+    table = pltpu.SMEM((2, half), jnp.int32)
+    packed, kind, index, limit = pl.pallas_call(
+        functools.partial(pack_kernel, n, slots, sub, block_len),
+        out_shape=(jax.ShapeDtypeStruct(slot_shape, BF16), lists, lists, lists),
+        in_specs=[SMEM, ANY], out_specs=(VMEM, SMEM, SMEM, SMEM),
+        scratch_shapes=[table] * 4 + [pltpu.SemaphoreType.DMA((2, half))],
+        compiler_params=params(SMALL),
+    )(meta, grid_field)
 
     def exchange(i, low, high, *args):
         return pl.pallas_call(
@@ -319,33 +410,14 @@
             ),
             in_specs=[ANY] * 3, out_specs=(ANY,) * 3,
             scratch_shapes=[pltpu.SemaphoreType.DMA((4,)), pltpu.SemaphoreType.DMA((4,))],
-            compiler_params=params(collective_id=i, has_side_effects=True),
+            compiler_params=params(SMALL, collective_id=i, has_side_effects=True),
         )(*args)
 
     received, embed_other, eo_other = lax.switch(
-        choice,
+        choice[0, 0],
         [functools.partial(exchange, i, low, high) for i, (low, high) in enumerate(sizes)],
         packed, embed_weight, edge_out_weight,
     )
-
-    mine = lax.dynamic_index_in_dim(rel, b, 0, False)
-    my_rank = lax.dynamic_index_in_dim(rank, b, 0, False)
-    my_need = lax.dynamic_index_in_dim(need, b, 0, False)
-    live_slot = lax.iota(jnp.int32, slots) < block_count[0]
-    is_low, is_high = mine < half, mine >= half + sub
-    side = jnp.where(is_low, mine, mine - sub)
-    hit = side[:, None] == cand[None]
-    far_index = jnp.sum(jnp.where(hit, my_rank.reshape(1, -1), 0), axis=1)
-    far_need = jnp.sum(jnp.where(hit, my_need.reshape(1, -1), 0), axis=1) > 0
-    far = (is_low | is_high) & far_need & live_slot
-    kind = jnp.where(far, jnp.where(is_low, 1, 2), 0).astype(jnp.int32)
-    local = jnp.clip(mine - half, 0, sub - 1)
-    index = jnp.where(far, far_index, local).astype(jnp.int32)
-    owner_live = jnp.where(is_low, live[down], jnp.where(is_high, live[up], band_points[0]))
-    inner = jnp.where(is_low, mine + half, jnp.where(is_high, mine - half - sub, mine - half))
-    limit = jnp.clip(owner_live - inner * block_len, 0, block_len)
-    reachable = live_slot & (far | ~(is_low | is_high))
-    limit = jnp.where(reachable, limit, 0).astype(jnp.int32)
 
     part = pl.pallas_call(
         functools.partial(remap_kernel, slots, width),
@@ -357,7 +429,7 @@
             pltpu.SemaphoreType.DMA((slots,)),
             pltpu.SemaphoreType.DMA((slots,)),
         ],
-        compiler_params=params(),
+        compiler_params=params(SMALL),
     )(kind, index, limit, grid_field, received, block_weight[0])
 
     ext = pl.pallas_call(
@@ -369,7 +441,7 @@
             pltpu.VMEM((3, nodes, channels), BF16),
             pltpu.SemaphoreType.DMA((3,)), pltpu.SemaphoreType.DMA((3,)),
         ],
-        compiler_params=params(collective_id=len(sizes), has_side_effects=True),
+        compiler_params=params(SMALL, collective_id=len(sizes), has_side_effects=True),
     )(part)
 
     edges = edge_src.shape[0]
@@ -386,7 +458,7 @@
             pltpu.VMEM((hid, 4 * nodes), BF16),
             pltpu.VMEM((nodes, hid), F32),
         ],
-        compiler_params=params(),
+        compiler_params=params(LARGE),
     )(ext, embed_weight, embed_other, edge_src.reshape(1, -1), edge_dst.reshape(1, -1), edge_in_weight)
 
     return pl.pallas_call(
@@ -399,7 +471,7 @@
             pltpu.VMEM((nodes, hid), BF16),
             pltpu.SemaphoreType.DMA((2,)), pltpu.SemaphoreType.DMA((2,)),
         ],
-        compiler_params=params(collective_id=len(sizes) + 1, has_side_effects=True),
+        compiler_params=params(LARGE, collective_id=len(sizes) + 1, has_side_effects=True),
     )(agg, initial, edge_out_weight, eo_other, node_in_weight, node_out_weight)
 
 

time: 90.5 us -> 61.6 us (0.68)
  blocking collectives: 16.2 us -> 0 us
  between operations: 8.84 us -> 1.55 us
  other arithmetic: 6.96 us -> 0 us
  Pallas kernels: 52.9 us -> 54.8 us
    unnamed x1 -> x0, blocking collectives: 16.2 us -> none
    pallas_call x1 -> x2, Pallas kernels: 2.05 us -> 12.7 us  [the longest x1 9.84 us: on_device(): pl.pallas_call(functools.partial(meta_kernel, n, slots, sub, block_len, s...]
    pallas_call x1, Pallas kernels: 14.7 us -> 9.59 us  [on_device(): pl.pallas_call(functools.partial(edge_kernel, chunk), out_shape=(jax.Shap...]
    pallas_call x1, Pallas kernels: 7.08 us -> 4.3 us  [on_device(): pl.pallas_call(node_kernel, out_shape=jax.ShapeDtypeStruct((nodes, hid),...]
    unnamed x9 -> x29, local copies, waits for them, and re-layouts: 2.93 us -> 5.55 us
    select_n x8 -> x0, other arithmetic: 2.46 us -> none  [the longest x1 1.82 us: on_device(): limit = jnp.where(reachable, limit, 0).astype(jnp.int32)]
    slice x4 -> x0, local copies, waits for them, and re-layouts: 1.63 us -> none  [the longest x2 0.85 us: on_device(): below = jnp.concatenate([live[:1], live[:-1]])]
    concatenate x2 -> x0, other arithmetic: 1.48 us -> none  [the longest x1 0.76 us: on_device(): above = jnp.concatenate([live[1:], live[-1:]])]
where the time goes in v2:
time: 61.6 us; the launch traced here: 61.9 us
  Pallas kernels  54.8 us (89%)
  local copies, waits for them, and re-layouts  5.55 us (9%)
  between operations  1.55 us (3%)
    pallas_call x1, Pallas kernels, exchange(): pl.pallas_call(functools.partial(exchange_kernel, n, low, high), out_shap...  16.7 us
    pallas_call x1, Pallas kernels, on_device(): pl.pallas_call(functools.partial(meta_kernel, n, slots, sub, block_len, s...  9.84 us
    pallas_call x1, Pallas kernels, on_device(): pl.pallas_call(functools.partial(edge_kernel, chunk), out_shape=(jax.Shap...  9.59 us
    pallas_call x1, Pallas kernels, on_device(): pl.pallas_call(functools.partial(share_kernel, n), out_shape=jax.ShapeDty...  7.35 us
    unnamed x29, local copies, waits for them, and re-layouts  5.55 us
    pallas_call x1, Pallas kernels, on_device(): pl.pallas_call(node_kernel, out_shape=jax.ShapeDtypeStruct((nodes, hid),...  4.3 us
    pallas_call x1, Pallas kernels, on_device(): pl.pallas_call(functools.partial(remap_kernel, slots, width), out_shape=j...  4.08 us
    pallas_call x1, Pallas kernels, on_device(): pl.pallas_call(functools.partial(pack_kernel, n, slots, sub, block_len),...  2.9 us

profile of v2, /device:TPU:0, one launch (start us, length us, event | category | flops | bytes accessed | tf_op | source)
XLA Modules:
  0.0 61.9 jit_solution(17452693299354624641)
XLA Ops:
  1.3 0.0 copy-start.8
  1.3 0.6 %copy-done.8 = s32[1,16]{1,0:T(1,128)S(1)} copy-done((s32[1,16]{1,0:T(1,128)S(1)}, s32[1,16]{1,0:T(1,128)}, u32[]{:S(2)}) %copy-start.8) | copy-done | bytes 88
  2.0 9.8 %shard_map.118 = (s32[16,1,128]{2,1,0:T(1,128)S(1)}, s32[1,128]{1,0:T(1,128)S(1)}) custom-call(s32[1,16]{1,0:T(1,128)S(1)} %copy-done.8, s32[1]{0:T(128)S(6)} %copy.36.count, s32[1]{0:T(128)S(6)} %copy.35.live), custom_call_target="tpu_custom_call" | custom-call | tf_op jit(solution)/shard_map/pallas_call | solution.py:377
  11.8 0.0 copy-start
  11.8 2.0 %copy-done = bf16[100,16384]{1,0:T(8,128)(2,1)S(1)} copy-done((bf16[100,16384]{1,0:T(8,128)(2,1)S(1)}, bf16[100,16384]{1,0:T(8,128)(2,1)}, u32[]{:S(2)}) %copy-start) | copy-done | bytes 3276824
  13.8 0.0 copy-start.9
  13.8 0.0 copy-start.11
  13.8 2.9 %shard_map.119 = (bf16[2,16,100,256]{3,2,1,0:T(8,128)(2,1)S(1)}, s32[16]{0:T(128)S(1)}, s32[16]{0:T(128)S(1)}, s32[16]{0:T(128)S(1)}) custom-call(s32[16,1,128]{2,1,0:T(1,128)S(1)} %get-tuple-element.79.meta, bf16[100,16384]{1,0:T(8,128)(2,1)S(1)} %copy-done), custom_call_target="tpu_custom_call" | custom-call | tf_op jit(solution)/shard_map/pallas_call | solution.py:395
  16.7 0.0 copy-done.9
  16.7 0.0 copy-done.11
  16.7 0.0 copy-start.1
  16.7 16.8 %conditional.1 = ((bf16[2,16,100,256]{3,2,1,0:T(8,128)(2,1)}, bf16[100,512]{1,0:T(8,128)(2,1)}, bf16[512,1024]{1,0:T(8,128)(2,1)})) conditional(s32[]{:T(128)} %bitcast, (bf16[2,16,100,256]{3,2,1,0:T(8,128)(2,1)S(1)}, bf16[100,512]{1,0:T(8,128)(2,1)S(1)}, bf16[512,1024]{1,0:T(8,128)(2,1)S(1)}) %tuple.48, ...), branch_computations={%region_0.0_spmd, %region_1.0_spmd, %region_2.0_spmd, %region_3.0_... | conditional | bytes 8 | solution.py:416
  16.8 16.7 %branch_3_fun.1 = (bf16[2,16,100,256]{3,2,1,0:T(8,128)(2,1)}, bf16[100,512]{1,0:T(8,128)(2,1)}, bf16[512,1024]{1,0:T(8,128)(2,1)}) custom-call(bf16[2,16,100,256]{3,2,1,0:T(8,128)(2,1)S(1)} %get-tuple-element.56.pk, bf16[100,512]{1,0:T(8,128)(2,1)S(1)} %get-tuple-element.57.emb, bf16[512,1024]{1,0:T(8,128)(2,1)S(1)} %get-tuple-element.58.eo), custom_call_target="tpu_custom_call" | custom-call | tf_op jit(solution)/shard_map/cond/branch_3_fun/pallas_call | solution.py:404
  33.5 0.0 copy-done.1
  33.5 0.0 copy-start.2
  33.5 2.2 %copy-done.2 = bf16[1,16,256,512]{3,2,1,0:T(8,128)(2,1)S(1)} copy-done((bf16[1,16,256,512]{3,2,1,0:T(8,128)(2,1)S(1)}, bf16[1,16,256,512]{3,2,1,0:T(8,128)(2,1)}, u32[]{:S(2)}) %copy-start.2) | copy-done | bytes 4194328
  35.7 0.0 copy-start.4
  35.7 0.0 copy-start.6
  35.7 0.0 copy-start.7
  35.7 0.0 copy-start.13
  35.7 0.0 copy-start.5
  35.7 0.0 copy-start.10
  35.8 0.0 copy-start.12
  35.8 4.1 %shard_map.120.part = f32[256,100]{1,0:T(8,128)S(1)} custom-call(s32[16]{0:T(128)S(1)} %get-tuple-element.80.kind_ref, s32[16]{0:T(128)S(1)} %get-tuple-element.81.index_ref, s32[16]{0:T(128)S(1)} %get-tuple-element.82.limit_ref, bf16[100,16384]{1,0:T(8,128)(2,1)S(1)} %copy-done.1, bf16[2,16,100,256]{3,2,1,0:T(8,128)(2,1)} %get-tuple-element.85.rv_ref, ...), custom_call_target="tpu_custom_call" | custom-call | tf_op jit(solution)/shard_map/pallas_call | solution.py:422
  39.9 0.0 copy-start.3
  39.9 7.3 %shard_map.121.ext = bf16[3,256,100]{2,1,0:T(8,128)(2,1)S(1)} custom-call(f32[256,100]{1,0:T(8,128)S(1)} %shard_map.120.part), custom_call_target="tpu_custom_call" | custom-call | tf_op jit(solution)/shard_map/pallas_call | solution.py:435
  47.2 0.0 copy-done.4
  47.2 0.0 copy-done.6
  47.2 0.0 copy-done.7
  47.3 0.0 copy-done.13
  47.3 9.6 %shard_map.122 = (bf16[256,512]{1,0:T(8,128)(2,1)S(1)}, bf16[256,1024]{1,0:T(8,128)(2,1)S(1)}) custom-call(bf16[3,256,100]{2,1,0:T(8,128)(2,1)S(1)} %shard_map.121.ext, bf16[100,512]{1,0:T(8,128)(2,1)S(1)} %copy-done.11, bf16[100,512]{1,0:T(8,128)(2,1)S(1)} %copy-done.13, s32[1,5120]{1,0:T(1,128)S(1)} %bitcast.6, s32[1,5120]{1,0:T(1,128)S(1)} %bitcast.7, ...), custom_call_target="tpu_custom_call" | custom-call | tf_op jit(solution)/shard_map/pallas_call | solution.py:449
  56.9 0.0 copy-done.5
  56.9 0.0 copy-done.10
  56.9 0.0 copy-done.12
  56.9 0.0 copy-done.3
  56.9 4.3 %shard_map.123 = bf16[256,512]{1,0:T(8,128)(2,1)S(1)} custom-call(bf16[256,512]{1,0:T(8,128)(2,1)S(1)} %get-tuple-element.87.agg, bf16[256,1024]{1,0:T(8,128)(2,1)S(1)} %get-tuple-element.88.init, bf16[512,1024]{1,0:T(8,128)(2,1)S(1)} %copy-done.10, bf16[512,1024]{1,0:T(8,128)(2,1)S(1)} %copy-done.12, bf16[2,1024,512]{2,1,0:T(8,128)(2,1)S(1)} %copy-done.3, ...), custom_call_target="tpu_custom_call" | custom-call | tf_op jit(solution)/shard_map/pallas_call | solution.py:464
  61.2 0.7 %copy.37 = bf16[256,512]{1,0:T(8,128)(2,1)} copy(bf16[256,512]{1,0:T(8,128)(2,1)S(1)} %shard_map.123) | data formatting | bytes 524288
Async XLA Ops:
  1.3 0.7 %copy-start.8 = (s32[1,16]{1,0:T(1,128)S(1)}, s32[1,16]{1,0:T(1,128)}, u32[]{:S(2)}) copy-start(s32[1,16]{1,0:T(1,128)} %ids.1) | copy-start | bytes 196
  11.8 2.0 %copy-start = (bf16[100,16384]{1,0:T(8,128)(2,1)S(1)}, bf16[100,16384]{1,0:T(8,128)(2,1)}, u32[]{:S(2)}) copy-start(bf16[100,16384]{1,0:T(8,128)(2,1)} %grid_ref.3) | copy-start | bytes 9830404
  13.8 2.9 %copy-start.9 = (bf16[512,1024]{1,0:T(8,128)(2,1)S(1)}, bf16[512,1024]{1,0:T(8,128)(2,1)}, u32[]{:S(2)}) copy-start(bf16[512,1024]{1,0:T(8,128)(2,1)} %eo.1) | copy-start | bytes 3145732
  13.8 2.9 %copy-start.11 = (bf16[100,512]{1,0:T(8,128)(2,1)S(1)}, bf16[100,512]{1,0:T(8,128)(2,1)}, u32[]{:S(2)}) copy-start(bf16[100,512]{1,0:T(8,128)(2,1)} %emb.1) | copy-start | bytes 307204
  16.7 16.8 %copy-start.1 = (bf16[100,16384]{1,0:T(8,128)(2,1)S(1)}, bf16[100,16384]{1,0:T(8,128)(2,1)}, u32[]{:S(2)}) copy-start(bf16[100,16384]{1,0:T(8,128)(2,1)} %grid_ref.3) | copy-start | bytes 9830404
  33.5 2.2 %copy-start.2 = (bf16[1,16,256,512]{3,2,1,0:T(8,128)(2,1)S(1)}, bf16[1,16,256,512]{3,2,1,0:T(8,128)(2,1)}, u32[]{:S(2)}) copy-start(bf16[1,16,256,512]{3,2,1,0:T(8,128)(2,1)} %param.23) | copy-start | bytes 12582916
  35.7 11.5 %copy-start.4 = (bf16[2,1024,512]{2,1,0:T(8,128)(2,1)S(1)}, bf16[2,1024,512]{2,1,0:T(8,128)(2,1)}, u32[]{:S(2)}) copy-start(bf16[2,1024,512]{2,1,0:T(8,128)(2,1)} %win.1) | copy-start | bytes 6291460
  35.7 11.5 %copy-start.6 = (s32[5120]{0:T(1024)S(1)}, s32[5120]{0:T(1024)}, u32[]{:S(2)}) copy-start(s32[5120]{0:T(1024)} %param.25) | copy-start | bytes 61444
  35.7 11.5 %copy-start.7 = (s32[5120]{0:T(1024)S(1)}, s32[5120]{0:T(1024)}, u32[]{:S(2)}) copy-start(s32[5120]{0:T(1024)} %param.26) | copy-start | bytes 61444
  35.7 11.5 %copy-start.13 = (bf16[100,512]{1,0:T(8,128)(2,1)S(1)}, bf16[100,512]{1,0:T(8,128)(2,1)}, u32[]{:S(2)}) copy-start(bf16[100,512]{1,0:T(8,128)(2,1)} %get-tuple-element.86.emb_o) | copy-start | bytes 307204
  35.7 21.1 %copy-start.5 = (bf16[512,1024]{1,0:T(8,128)(2,1)S(1)}, bf16[512,1024]{1,0:T(8,128)(2,1)}, u32[]{:S(2)}) copy-start(bf16[512,1024]{1,0:T(8,128)(2,1)} %nout.1) | copy-start | bytes 3145732
  35.7 21.1 %copy-start.10 = (bf16[512,1024]{1,0:T(8,128)(2,1)S(1)}, bf16[512,1024]{1,0:T(8,128)(2,1)}, u32[]{:S(2)}) copy-start(bf16[512,1024]{1,0:T(8,128)(2,1)} %eo.1) | copy-start | bytes 3145732
  35.8 21.1 %copy-start.12 = (bf16[512,1024]{1,0:T(8,128)(2,1)S(1)}, bf16[512,1024]{1,0:T(8,128)(2,1)}, u32[]{:S(2)}) copy-start(bf16[512,1024]{1,0:T(8,128)(2,1)} %get-tuple-element.89.eo_o) | copy-start | bytes 3145732
  39.9 17.0 %copy-start.3 = (bf16[2,1024,512]{2,1,0:T(8,128)(2,1)S(1)}, bf16[2,1024,512]{2,1,0:T(8,128)(2,1)}, u32[]{:S(2)}) copy-start(bf16[2,1024,512]{2,1,0:T(8,128)(2,1)} %nin.1) | copy-start | bytes 6291460
